TPU v7x, 32 devices: a whole 2x2x4 slice. The times are simulated.
32 devices in a mesh: row: 8 (over z, y), ch: 4 (over x, core).
Axes of the slice: x: 2, y: 2, z: 4, core: 2. Of those that a mesh axis runs over, the one named last changes fastest.
Arguments:
- pair_rep: float32 [64, 64, 128], P(('row', 'ch')), may hold values from -6 to 6
- pair_mask: int32 [64, 64], P(('row', 'ch')), may hold values from 0 to 1, as said below
- ln_in_gain: float32 [128], replicated, may hold values from 0.5 to 1.5
- ln_in_bias: float32 [128], replicated, may hold values from -3 to 3
- w_in: float32 [128, 640], replicated, may hold values from -0.5 to 0.5
- b_in: float32 [640], replicated, may hold values from -3 to 3
- ln_out_gain: float32 [128], replicated, may hold values from 0.5 to 1.5
- ln_out_bias: float32 [128], replicated, may hold values from -3 to 3
- w_out: float32 [128, 128], replicated, may hold values from -0.5 to 0.5
- b_out: float32 [128], replicated, may hold values from -3 to 3
- cotangent: float32 [64, 64, 128], P(('row', 'ch')), may hold values from -6 to 6
Outputs:
- update: float32 [64, 64, 128], P(('row', 'ch'))
- grad_pair: float32 [64, 64, 128], P(('row', 'ch'))
- grad_w_in: float32 [128, 640], replicated
- grad_w_out: float32 [128, 128], replicated
Inputs may be any that keep to these rules, and one draw needn't show every extreme that they name: pair_mask[i, k] = m_i m_k, where m is 1 for the residues present in the crop and 0 otherwise.
All inputs are finite; a program needn't handle non-finite values.
Results may differ from a plain program's by a relative error of at most 0.00009.
Values sent between devices are 32-bit elements; how exact they have to be, the bound alone decides.
A program may use at most 64 MiB of HBM per device.

v0:
```python
import functools

import jax
import jax.numpy as jnp
from jax import lax
from jax.experimental import pallas as pl
from jax.experimental.pallas import tpu as pltpu
from jax.sharding import PartitionSpec as P

epsilon = 1e-05
MESH = pl.DeviceIdType.MESH


def halves(a):
    high = a.astype(jnp.bfloat16)
    return high, (a - high.astype(jnp.float32)).astype(jnp.bfloat16)


def dot(a, b, contract):
    def one(x, y):
        return lax.dot_general(
            x, y, (contract, ((), ())), preferred_element_type=jnp.float32
        )

    a_high, a_low = halves(a)
    b_high, b_low = halves(b)
    return one(a_high, b_low) + one(a_low, b_high) + one(a_high, b_high)


NN = ((1,), (0,))
NT = ((1,), (1,))
TN = ((0,), (0,))


def normalise(x):
    center = jnp.mean(x, -1, keepdims=True)
    spread = jnp.mean((x - center) ** 2, -1, keepdims=True)
    scale = lax.rsqrt(spread + epsilon)
    return (x - center) * scale, scale


def normalise_back(x_hat, scale, d_hat):
    return scale * (
        d_hat
        - jnp.mean(d_hat, -1, keepdims=True)
        - x_hat * jnp.mean(d_hat * x_hat, -1, keepdims=True)
    )


def kernel(
    n_row,
    n_ch,
    *refs,
):
    inputs, rest = refs[:11], refs[11:]
    update_out, gpair_out, recv6, recv8, recv11 = rest[:5]
    held, rest = rest[5:16], rest[16:]
    (
        pair_ref,
        mask_ref,
        gin_ref,
        bin_ref,
        win_ref,
        b_ref,
        gout_ref,
        bout_ref,
        wout_ref,
        bo_ref,
        cot_ref,
    ) = held
    (
        update_ref,
        gpair_ref,
        send1,
        recv1,
        send2,
        recv2,
        send3,
        recv3,
        send4,
        recv4,
        send5,
        recv5,
        send6,
        send7,
        recv7,
        send8,
        send9,
        recv9,
        send10,
        recv10,
        send11,
        send_sems,
        recv_sems,
        load_sems,
        store_sems,
    ) = rest
    n = n_row * n_ch
    rows, length, channels = pair_ref.shape
    hidden = wout_ref.shape[0]
    own = hidden // n
    cells = rows * length
    my_row = lax.axis_index("row")
    my_ch = lax.axis_index("ch")
    me = my_row * n_ch + my_ch

    barrier = pltpu.get_barrier_semaphore()

    def greet(t, carry):
        d = lax.rem(me + t, n)
        pl.semaphore_signal(
            barrier, inc=1, device_id=(d // n_ch, lax.rem(d, n_ch)), device_id_type=MESH
        )
        return carry

    lax.fori_loop(1, n, greet, 0)

    loads = [
        pltpu.make_async_copy(inputs[k], held[k], load_sems.at[k]) for k in range(len(inputs))
    ]
    for k in (0, 2, 3, 4, 5, 1, 10, 6, 7, 8, 9):
        loads[k].start()

    def exchange(phase, src, dst, spread):
        def one(t, carry):
            d = lax.rem(me + t, n)
            pltpu.make_async_remote_copy(
                src_ref=src.at[d] if spread else src,
                dst_ref=dst.at[me],
                send_sem=send_sems.at[phase],
                recv_sem=recv_sems.at[phase],
                device_id=(d // n_ch, lax.rem(d, n_ch)),
                device_id_type=MESH,
            ).start()
            return carry

        lax.fori_loop(1, n, one, 0)
        if spread:
            dst[me] = src[me]

    def arrived(phase, dst):
        part = dst.at[pl.ds(0, n - 1)]
        pltpu.make_async_copy(part, part, recv_sems.at[phase]).wait()

    def sent(phase, dst):
        part = dst.at[pl.ds(0, n - 1)]
        pltpu.make_async_copy(part, part, send_sems.at[phase]).wait()

    def load_cells(ref):
        return jnp.concatenate(
            [ref[i, pl.ds(p, n, stride=rows), :] for i in range(rows) for p in range(rows)], 0
        )

    def store_cells(ref, value):
        for i in range(rows):
            for p in range(rows):
                at = i * length + p * n
                ref[i, pl.ds(p, n, stride=rows), :] = value[at : at + n]

    def split_h(value):
        return value.T.reshape(n, own, cells)

    def merge_h(value):
        return value.reshape(hidden, cells).T

    def stack(value):
        return jnp.concatenate([value[:, i * length : (i + 1) * length] for i in range(rows)], 0)

    def unstack(value):
        return jnp.concatenate([value[i * n : (i + 1) * n] for i in range(rows)], 1)

    def bias(first, last):
        return jnp.concatenate([b_ref[k : k + 1] for k in range(first, last)], 1)

    natural = lax.broadcasted_iota(jnp.int32, (length, length), 0)
    place = lax.broadcasted_iota(jnp.int32, (length, length), 1)
    order = jnp.where(natural == lax.rem(place, n) * rows + place // n, 1.0, 0.0)
    loads[1].wait()
    keep = lax.dot_general(
        mask_ref[...].astype(jnp.bfloat16),
        order.astype(jnp.bfloat16),
        (NN, ((), ())),
        preferred_element_type=jnp.float32,
    )
    keep = jnp.concatenate([keep[i : i + 1] for i in range(rows)], 1)

    loads[0].wait()
    loads[2].wait()
    loads[3].wait()
    pair_hat, pair_scale = normalise(load_cells(pair_ref))
    normed = pair_hat * gin_ref[...] + bin_ref[...]
    width = 4 * hidden
    lanes = b_ref.shape[1]
    loads[4].wait()
    loads[5].wait()
    pieces = dot(normed, win_ref[:, :width], NN) + bias(0, width // lanes)
    p1 = jax.nn.sigmoid(pieces[:, :hidden])
    p2 = pieces[:, hidden : 2 * hidden]
    p3 = jax.nn.sigmoid(pieces[:, 2 * hidden : 3 * hidden])
    p4 = pieces[:, 3 * hidden :]
    keep_tall = jnp.broadcast_to(keep, (hidden, cells)).T
    left = keep_tall * p1 * p2
    right = keep_tall * p3 * p4
    send1[:, :own, :] = split_h(left)
    send1[:, own:, :] = split_h(right)
    pl.semaphore_wait(barrier, n - 1)
    exchange(0, send1, recv1, True)

    gate = jax.nn.sigmoid(dot(normed, win_ref[:, width:], NN) + bias(width // lanes, b_ref.shape[0]))
    for k in range(6, 11):
        loads[k].wait()
    cot = load_cells(cot_ref)

    arrived(0, recv1)
    lefts = [stack(recv1[:, h, :]) for h in range(own)]
    rights = [stack(recv1[:, own + h, :]) for h in range(own)]
    for h in range(own):
        send2[:, h, :] = unstack(dot(lefts[h], rights[h], NT))
    exchange(1, send2, recv2, True)
    arrived(1, recv2)

    prod_hat, prod_scale = normalise(merge_h(recv2[...]))
    normed_product = prod_hat * gout_ref[...] + bout_ref[...]
    projected = dot(normed_product, wout_ref[...], NN) + bo_ref[...]
    d_out = cot * gate
    d_product = normalise_back(
        prod_hat, prod_scale, dot(d_out, wout_ref[...], NT) * gout_ref[...]
    )
    send3[...] = split_h(d_product)
    exchange(2, send3, recv3, True)

    store_cells(update_ref, gate * projected)
    update_copy = pltpu.make_async_copy(update_ref, update_out, store_sems.at[0])
    update_copy.start()
    d_gate = cot * projected * gate * (1.0 - gate)
    d_wout = dot(normed_product, d_out, TN)
    d_wgate = dot(normed, d_gate, TN)
    send4[...] = jnp.concatenate([d_wgate, d_wout], 1).reshape(n, own, channels + channels)
    exchange(3, send4, recv4, True)
    d_normed = dot(d_gate, win_ref[:, width:], NT)

    arrived(2, recv3)
    d_cols = [stack(recv3[:, h, :]) for h in range(own)]
    for h in range(own):
        send5[:, h, :] = unstack(dot(d_cols[h], rights[h], NN))
    exchange(4, send5, recv5, True)
    for h in range(own):
        send9[:, h, :] = unstack(dot(d_cols[h], lefts[h], TN))
    exchange(8, send9, recv9, True)

    arrived(3, recv4)
    send6[...] = jnp.sum(recv4[...], 0) / length
    early_copy = pltpu.make_async_copy(send6, recv6.at[me], store_sems.at[2])
    early_copy.start()
    exchange(5, send6, recv6, False)

    arrived(4, recv5)
    half = 2 * hidden
    d_left = merge_h(recv5[...]) * keep_tall
    d_first = jnp.concatenate([d_left * p2 * p1 * (1.0 - p1), d_left * p1], 1)
    send7[...] = dot(normed, d_first, TN).reshape(n, own, half)
    exchange(6, send7, recv7, True)
    d_normed = d_normed + dot(d_first, win_ref[:, :half], NT)
    arrived(8, recv9)
    d_right = merge_h(recv9[...]) * keep_tall
    d_second = jnp.concatenate([d_right * p4 * p3 * (1.0 - p3), d_right * p3], 1)
    send10[...] = dot(normed, d_second, TN).reshape(n, own, half)
    exchange(9, send10, recv10, True)
    d_normed = d_normed + dot(d_second, win_ref[:, half:width], NT)
    store_cells(gpair_ref, normalise_back(pair_hat, pair_scale, d_normed * gin_ref[...]))
    gpair_copy = pltpu.make_async_copy(gpair_ref, gpair_out, store_sems.at[1])
    gpair_copy.start()
    arrived(6, recv7)
    send8[...] = jnp.sum(recv7[...], 0) / length
    exchange(7, send8, recv8, False)
    late_copy = pltpu.make_async_copy(send8, recv8.at[me], store_sems.at[3])
    late_copy.start()
    arrived(9, recv10)
    send11[...] = jnp.sum(recv10[...], 0) / length
    exchange(10, send11, recv11, False)
    last_copy = pltpu.make_async_copy(send11, recv11.at[me], store_sems.at[4])
    last_copy.start()

    arrived(5, recv6)
    arrived(7, recv8)
    arrived(10, recv11)
    for copy in (update_copy, gpair_copy, early_copy, late_copy, last_copy):
        copy.wait()
    sent(0, recv1)
    sent(1, recv2)
    sent(2, recv3)
    sent(3, recv4)
    sent(4, recv5)
    sent(5, recv6)
    sent(6, recv7)
    sent(7, recv8)
    sent(8, recv9)
    sent(9, recv10)
    sent(10, recv11)


def finish(update, gpair, early, late, last, update_ref, gpair_ref, gwin_ref, gwout_ref):
    channels = gwin_ref.shape[0]
    width = late.shape[2]
    update_ref[...] = update[...]
    gpair_ref[...] = gpair[...]
    early_rows = early[...].reshape(channels, 2 * channels)
    gwin_ref[:, 2 * width :] = early_rows[:, :channels]
    gwout_ref[...] = early_rows[:, channels:]
    gwin_ref[:, :width] = late[...].reshape(channels, width)
    gwin_ref[:, width : 2 * width] = last[...].reshape(channels, width)


def on_device(
    n_row,
    n_ch,
    pair_rep,
    pair_mask,
    ln_in_gain,
    ln_in_bias,
    w_in,
    b_in,
    ln_out_gain,
    ln_out_bias,
    w_out,
    b_out,
    cotangent,
):
    n = n_row * n_ch
    rows, length, channels = pair_rep.shape
    hidden = w_out.shape[0]
    own = hidden // n
    cells = rows * length
    f32 = jnp.float32

    def both(*shape):
        return [pltpu.VMEM((n, *shape), f32), pltpu.VMEM((n, *shape), f32)]

    inputs = (
        pair_rep,
        pair_mask,
        ln_in_gain[None],
        ln_in_bias[None],
        w_in,
        b_in.reshape(-1, min(128, hidden)),
        ln_out_gain[None],
        ln_out_bias[None],
        w_out,
        b_out[None],
        cotangent,
    )
    anywhere = pl.BlockSpec(memory_space=pl.ANY)
    parts = pl.pallas_call(
        functools.partial(kernel, n_row, n_ch),
        out_shape=(
            jax.ShapeDtypeStruct(pair_rep.shape, f32),
            jax.ShapeDtypeStruct(pair_rep.shape, f32),
            jax.ShapeDtypeStruct((n, own, 2 * channels), f32),
            jax.ShapeDtypeStruct((n, own, 2 * hidden), f32),
            jax.ShapeDtypeStruct((n, own, 2 * hidden), f32),
        ),
        in_specs=[anywhere] * 11,
        out_specs=(anywhere,) * 5,
        scratch_shapes=[
            *[pltpu.VMEM(x.shape, x.dtype) for x in inputs],
            pltpu.VMEM(pair_rep.shape, f32),
            pltpu.VMEM(pair_rep.shape, f32),
            *both(2 * own, cells),
            *both(own, cells),
            *both(own, cells),
            *both(own, 2 * channels),
            *both(own, cells),
            pltpu.VMEM((own, 2 * channels), f32),
            *both(own, 2 * hidden),
            pltpu.VMEM((own, 2 * hidden), f32),
            *both(own, cells),
            *both(own, 2 * hidden),
            pltpu.VMEM((own, 2 * hidden), f32),
            pltpu.SemaphoreType.DMA((11,)),
            pltpu.SemaphoreType.DMA((11,)),
            pltpu.SemaphoreType.DMA((11,)),
            pltpu.SemaphoreType.DMA((5,)),
        ],
        compiler_params=pltpu.CompilerParams(collective_id=0, has_side_effects=True),
    )(*inputs)
    vmem = pl.BlockSpec(memory_space=pltpu.VMEM)
    return pl.pallas_call(
        finish,
        out_shape=(
            jax.ShapeDtypeStruct(pair_rep.shape, f32),
            jax.ShapeDtypeStruct(pair_rep.shape, f32),
            jax.ShapeDtypeStruct(w_in.shape, f32),
            jax.ShapeDtypeStruct(w_out.shape, f32),
        ),
        in_specs=[vmem] * 5,
        out_specs=(vmem,) * 4,
    )(*parts)


def solution(mesh):
    rows = P(("row", "ch"), None, None)
    placed = (rows, P(("row", "ch"), None), P(), P(), P(), P(), P(), P(), P(), P(), rows)
    return jax.shard_map(
        functools.partial(on_device, mesh.shape["row"], mesh.shape["ch"]),
        mesh=mesh,
        in_specs=placed,
        out_specs=(rows, rows, P(), P()),
        check_vma=False,
    )
```

profile of v0, /device:TPU:0, one launch (start us, length us, event | category | flops | bytes accessed | tf_op | source)
XLA Modules:
  0.0 45.7 jit_solution(8192625482696563051)
XLA Ops:
  0.6 43.1 %shard_map.138 = (f32[2,64,128]{2,1,0:T(8,128)}, f32[2,64,128]{2,1,0:T(8,128)}, f32[32,4,256]{2,1,0:T(4,128)}, f32[32,4,256]{2,1,0:T(4,128)}, f32[32,4,256]{2,1,0:T(4,128)}) custom-call(f32[2,64,128]{2,1,0:T(8,128)} %refs_0_.1, s32[2,64]{1,0:T(2,128)} %refs_1_.1, f32[1,128]{1,0:T(1,128)} %bitcast.7, f32[1,128]{1,0:T(1,128)} %bitcast.8, f32[128,640]{1,0:T(8,128)} %refs_4_.1, ...), custom_call_target="tpu_custom_call" | custom-call | tf_op jit(solution)/shard_map/pallas_call | solution.py:353
  43.8 1.9 %shard_map.139 = (f32[2,64,128]{2,1,0:T(8,128)}, f32[2,64,128]{2,1,0:T(8,128)}, f32[128,640]{1,0:T(8,128)}, f32[128,128]{1,0:T(8,128)}) custom-call(f32[2,64,128]{2,1,0:T(8,128)} %get-tuple-element.9.update, f32[2,64,128]{2,1,0:T(8,128)} %get-tuple-element.10.gpair, f32[32,4,256]{2,1,0:T(4,128)} %get-tuple-element.11.early, ...), custom_call_target="tpu_custom_call" | custom-call | tf_op jit(solution)/shard_map/pallas_call | solution.py:387
where the time goes:
time: 45.8 us; the launch traced here: 45.7 us
  Pallas kernels  45 us (98%)
  between operations  0.64 us (1%)
    pallas_call x1, Pallas kernels, on_device(): pl.pallas_call(functools.partial(kernel, n_row, n_ch), out_shape=(jax.Sha...  43.1 us
    pallas_call x1, Pallas kernels, on_device(): pl.pallas_call(finish, out_shape=(jax.ShapeDtypeStruct(pair_rep.shape, f3...  1.9 us

commit v1 on v0

--- a/solution.py
+++ b/solution.py
@@ -45,6 +45,16 @@
         - jnp.mean(d_hat, -1, keepdims=True)
         - x_hat * jnp.mean(d_hat * x_hat, -1, keepdims=True)
     )
+
+
+def farthest_first(n, n_ch):
+    assert n & (n - 1) == 0
+
+    def hops(t):
+        row, ch = divmod(t, n_ch)
+        return (row // 2).bit_length() + row % 2 + ch // 2
+
+    return sorted(range(1, n), key=lambda t: (hops(t), t), reverse=True)
 
 
 def kernel(
@@ -104,16 +114,15 @@
     my_ch = lax.axis_index("ch")
     me = my_row * n_ch + my_ch
 
+    peers = farthest_first(n, n_ch)
+
+    def place_of(t):
+        d = me ^ t
+        return d, (d // n_ch, lax.rem(d, n_ch))
+
     barrier = pltpu.get_barrier_semaphore()
-
-    def greet(t, carry):
-        d = lax.rem(me + t, n)
-        pl.semaphore_signal(
-            barrier, inc=1, device_id=(d // n_ch, lax.rem(d, n_ch)), device_id_type=MESH
-        )
-        return carry
-
-    lax.fori_loop(1, n, greet, 0)
+    for t in peers:
+        pl.semaphore_signal(barrier, inc=1, device_id=place_of(t)[1], device_id_type=MESH)
 
     loads = [
         pltpu.make_async_copy(inputs[k], held[k], load_sems.at[k]) for k in range(len(inputs))
@@ -122,19 +131,16 @@
         loads[k].start()
 
     def exchange(phase, src, dst, spread):
-        def one(t, carry):
-            d = lax.rem(me + t, n)
+        for t in peers:
+            d, place = place_of(t)
             pltpu.make_async_remote_copy(
                 src_ref=src.at[d] if spread else src,
                 dst_ref=dst.at[me],
                 send_sem=send_sems.at[phase],
                 recv_sem=recv_sems.at[phase],
-                device_id=(d // n_ch, lax.rem(d, n_ch)),
+                device_id=place,
                 device_id_type=MESH,
             ).start()
-            return carry
-
-        lax.fori_loop(1, n, one, 0)
         if spread:
             dst[me] = src[me]
 

time: 45.8 us -> 44.9 us (0.980)
  Pallas kernels: 45 us -> 44.1 us
    pallas_call x1, Pallas kernels: 43.1 us -> 42.2 us  [on_device(): pl.pallas_call(functools.partial(kernel, n_row, n_ch), out_shape=(jax.Sha...]
where the time goes in v1:
time: 44.9 us; the launch traced here: 44.8 us
  Pallas kernels  44.1 us (98%)
  between operations  0.64 us (1%)
    pallas_call x1, Pallas kernels, on_device(): pl.pallas_call(functools.partial(kernel, n_row, n_ch), out_shape=(jax.Sha...  42.2 us
    pallas_call x1, Pallas kernels, on_device(): pl.pallas_call(finish, out_shape=(jax.ShapeDtypeStruct(pair_rep.shape, f3...  1.9 us

profile of v1, /device:TPU:0, one launch (start us, length us, event | category | flops | bytes accessed | tf_op | source)
XLA Modules:
  0.0 44.8 jit_solution(3043270280852958362)
XLA Ops:
  0.6 42.2 %shard_map.138 = (f32[2,64,128]{2,1,0:T(8,128)}, f32[2,64,128]{2,1,0:T(8,128)}, f32[32,4,256]{2,1,0:T(4,128)}, f32[32,4,256]{2,1,0:T(4,128)}, f32[32,4,256]{2,1,0:T(4,128)}) custom-call(f32[2,64,128]{2,1,0:T(8,128)} %refs_0_.1, s32[2,64]{1,0:T(2,128)} %refs_1_.1, f32[1,128]{1,0:T(1,128)} %bitcast.7, f32[1,128]{1,0:T(1,128)} %bitcast.8, f32[128,640]{1,0:T(8,128)} %refs_4_.1, ...), custom_call_target="tpu_custom_call" | custom-call | tf_op jit(solution)/shard_map/pallas_call | solution.py:359
  42.9 1.9 %shard_map.139 = (f32[2,64,128]{2,1,0:T(8,128)}, f32[2,64,128]{2,1,0:T(8,128)}, f32[128,640]{1,0:T(8,128)}, f32[128,128]{1,0:T(8,128)}) custom-call(f32[2,64,128]{2,1,0:T(8,128)} %get-tuple-element.9.update, f32[2,64,128]{2,1,0:T(8,128)} %get-tuple-element.10.gpair, f32[32,4,256]{2,1,0:T(4,128)} %get-tuple-element.11.early, ...), custom_call_target="tpu_custom_call" | custom-call | tf_op jit(solution)/shard_map/pallas_call | solution.py:393

commit v2 on v1

--- a/solution.py
+++ b/solution.py
@@ -63,8 +63,8 @@
     *refs,
 ):
     inputs, rest = refs[:11], refs[11:]
-    update_out, gpair_out, recv6, recv8, recv11 = rest[:5]
-    held, rest = rest[5:16], rest[16:]
+    update_ref, gpair_ref, gwin_out, gwout_out = rest[:4]
+    held, rest = rest[4:15], rest[15:]
     (
         pair_ref,
         mask_ref,
@@ -79,8 +79,7 @@
         cot_ref,
     ) = held
     (
-        update_ref,
-        gpair_ref,
+        recv6, recv8, recv11,
         send1,
         recv1,
         send2,
@@ -236,8 +235,6 @@
     exchange(2, send3, recv3, True)
 
     store_cells(update_ref, gate * projected)
-    update_copy = pltpu.make_async_copy(update_ref, update_out, store_sems.at[0])
-    update_copy.start()
     d_gate = cot * projected * gate * (1.0 - gate)
     d_wout = dot(normed_product, d_out, TN)
     d_wgate = dot(normed, d_gate, TN)
@@ -256,8 +253,7 @@
 
     arrived(3, recv4)
     send6[...] = jnp.sum(recv4[...], 0) / length
-    early_copy = pltpu.make_async_copy(send6, recv6.at[me], store_sems.at[2])
-    early_copy.start()
+    recv6[me] = send6[...]
     exchange(5, send6, recv6, False)
 
     arrived(4, recv5)
@@ -274,24 +270,19 @@
     exchange(9, send10, recv10, True)
     d_normed = d_normed + dot(d_second, win_ref[:, half:width], NT)
     store_cells(gpair_ref, normalise_back(pair_hat, pair_scale, d_normed * gin_ref[...]))
-    gpair_copy = pltpu.make_async_copy(gpair_ref, gpair_out, store_sems.at[1])
-    gpair_copy.start()
     arrived(6, recv7)
     send8[...] = jnp.sum(recv7[...], 0) / length
     exchange(7, send8, recv8, False)
-    late_copy = pltpu.make_async_copy(send8, recv8.at[me], store_sems.at[3])
-    late_copy.start()
+    recv8[me] = send8[...]
     arrived(9, recv10)
     send11[...] = jnp.sum(recv10[...], 0) / length
     exchange(10, send11, recv11, False)
-    last_copy = pltpu.make_async_copy(send11, recv11.at[me], store_sems.at[4])
-    last_copy.start()
+    recv11[me] = send11[...]
 
     arrived(5, recv6)
     arrived(7, recv8)
     arrived(10, recv11)
-    for copy in (update_copy, gpair_copy, early_copy, late_copy, last_copy):
-        copy.wait()
+    finish(None, None, recv6, recv8, recv11, None, None, gwin_out, gwout_out)
     sent(0, recv1)
     sent(1, recv2)
     sent(2, recv3)
@@ -305,11 +296,17 @@
     sent(10, recv11)
 
 
+def write_out(a, b, c, d, ao, bo, co, do, sems):
+    cs = [pltpu.make_async_copy(x, y, sems.at[k]) for k, (x, y) in enumerate(((a, ao), (b, bo), (c, co), (d, do)))]
+    for x in cs:
+        x.start()
+    for x in cs:
+        x.wait()
+
+
 def finish(update, gpair, early, late, last, update_ref, gpair_ref, gwin_ref, gwout_ref):
     channels = gwin_ref.shape[0]
     width = late.shape[2]
-    update_ref[...] = update[...]
-    gpair_ref[...] = gpair[...]
     early_rows = early[...].reshape(channels, 2 * channels)
     gwin_ref[:, 2 * width :] = early_rows[:, :channels]
     gwout_ref[...] = early_rows[:, channels:]
@@ -356,21 +353,22 @@
         cotangent,
     )
     anywhere = pl.BlockSpec(memory_space=pl.ANY)
+    inputs = tuple(pltpu.with_memory_space_constraint(x, pltpu.MemorySpace.HBM) for x in inputs)
     parts = pl.pallas_call(
         functools.partial(kernel, n_row, n_ch),
         out_shape=(
             jax.ShapeDtypeStruct(pair_rep.shape, f32),
             jax.ShapeDtypeStruct(pair_rep.shape, f32),
-            jax.ShapeDtypeStruct((n, own, 2 * channels), f32),
-            jax.ShapeDtypeStruct((n, own, 2 * hidden), f32),
-            jax.ShapeDtypeStruct((n, own, 2 * hidden), f32),
+            jax.ShapeDtypeStruct(w_in.shape, f32),
+            jax.ShapeDtypeStruct(w_out.shape, f32),
         ),
         in_specs=[anywhere] * 11,
-        out_specs=(anywhere,) * 5,
+        out_specs=(pl.BlockSpec(memory_space=pltpu.VMEM),) * 4,
         scratch_shapes=[
             *[pltpu.VMEM(x.shape, x.dtype) for x in inputs],
-            pltpu.VMEM(pair_rep.shape, f32),
-            pltpu.VMEM(pair_rep.shape, f32),
+            pltpu.VMEM((n, own, 2 * channels), f32),
+            pltpu.VMEM((n, own, 2 * hidden), f32),
+            pltpu.VMEM((n, own, 2 * hidden), f32),
             *both(2 * own, cells),
             *both(own, cells),
             *both(own, cells),
@@ -387,19 +385,15 @@
             pltpu.SemaphoreType.DMA((11,)),
             pltpu.SemaphoreType.DMA((5,)),
         ],
-        compiler_params=pltpu.CompilerParams(collective_id=0, has_side_effects=True),
+        compiler_params=pltpu.CompilerParams(collective_id=0, has_side_effects=True, vmem_limit_bytes=24 << 20),
     )(*inputs)
-    vmem = pl.BlockSpec(memory_space=pltpu.VMEM)
     return pl.pallas_call(
-        finish,
-        out_shape=(
-            jax.ShapeDtypeStruct(pair_rep.shape, f32),
-            jax.ShapeDtypeStruct(pair_rep.shape, f32),
-            jax.ShapeDtypeStruct(w_in.shape, f32),
-            jax.ShapeDtypeStruct(w_out.shape, f32),
-        ),
-        in_specs=[vmem] * 5,
-        out_specs=(vmem,) * 4,
+        write_out,
+        out_shape=tuple(jax.ShapeDtypeStruct(x.shape, f32) for x in (pair_rep, pair_rep, w_in, w_out)),
+        in_specs=[pl.BlockSpec(memory_space=pltpu.VMEM)] * 4,
+        out_specs=(anywhere,) * 4,
+        scratch_shapes=[pltpu.SemaphoreType.DMA((4,))],
+        compiler_params=pltpu.CompilerParams(vmem_limit_bytes=8 << 20),
     )(*parts)
 
 

time: 44.9 us -> 43.8 us (0.976)
  Pallas kernels: 44.1 us -> 43 us
    pallas_call x1, Pallas kernels: 1.9 us -> 0.82 us  [on_device(): pl.pallas_call(write_out, out_shape=tuple((jax.ShapeDtypeStruct(x.shape,...]
where the time goes in v2:
time: 43.8 us; the launch traced here: 43.6 us
  Pallas kernels  43 us (98%)
  between operations  0.64 us (1%)
    pallas_call x1, Pallas kernels, on_device(): pl.pallas_call(functools.partial(kernel, n_row, n_ch), out_shape=(jax.Sha...  42.2 us

profile of v2, /device:TPU:0, one launch (start us, length us, event | category | flops | bytes accessed | tf_op | source)
XLA Modules:
  0.0 43.6 jit_solution(18246824915054520803)
XLA Ops:
  0.6 42.2 %shard_map.138 = (f32[2,64,128]{2,1,0:T(8,128)S(1)}, f32[2,64,128]{2,1,0:T(8,128)S(1)}, f32[128,640]{1,0:T(8,128)S(1)}, f32[128,128]{1,0:T(8,128)S(1)}) custom-call(f32[2,64,128]{2,1,0:T(8,128)} %refs_0_.1, s32[2,64]{1,0:T(2,128)} %refs_1_.1, f32[1,128]{1,0:T(1,128)} %bitcast.7, f32[1,128]{1,0:T(1,128)} %bitcast.8, f32[128,640]{1,0:T(8,128)} %refs_4_.1, ...), custom_call_target="tpu_custom_call" | custom-call | tf_op jit(solution)/shard_map/pallas_call | solution.py:357
  42.8 0.8 %shard_map.139 = (f32[2,64,128]{2,1,0:T(8,128)}, f32[2,64,128]{2,1,0:T(8,128)}, f32[128,640]{1,0:T(8,128)}, f32[128,128]{1,0:T(8,128)}) custom-call(f32[2,64,128]{2,1,0:T(8,128)S(1)} %get-tuple-element.8.a, f32[2,64,128]{2,1,0:T(8,128)S(1)} %get-tuple-element.9.b, f32[128,640]{1,0:T(8,128)S(1)} %get-tuple-element.10.c, f32[128,128]{1,0:T(8,128)S(1)} %get-tuple-element.11.d), custom_call_target="tpu_custom_call" | custom-call | tf_op jit(solution)/shard_map/pallas_call | solution.py:390

commit v3 on v2

--- a/solution.py
+++ b/solution.py
@@ -16,15 +16,18 @@
     return high, (a - high.astype(jnp.float32)).astype(jnp.bfloat16)
 
 
-def dot(a, b, contract):
+def dot_halves(a, b, contract):
     def one(x, y):
         return lax.dot_general(
             x, y, (contract, ((), ())), preferred_element_type=jnp.float32
         )
 
-    a_high, a_low = halves(a)
-    b_high, b_low = halves(b)
+    (a_high, a_low), (b_high, b_low) = a, b
     return one(a_high, b_low) + one(a_low, b_high) + one(a_high, b_high)
+
+
+def dot(a, b, contract):
+    return dot_halves(halves(a), halves(b), contract)
 
 
 NN = ((1,), (0,))
@@ -57,13 +60,41 @@
     return sorted(range(1, n), key=lambda t: (hops(t), t), reverse=True)
 
 
+def gather_plan(n, n_ch, rows):
+    core, side, up = 1, n_ch // 2, n_ch
+    middle = rows // 16 * 8
+    plan = []
+    for z in range(0, n, 2 * n_ch):
+        low = z & -z
+        stage = 0 if z == 0 else 1 if z == low else 2
+        if stage == 1:
+            plan.append((0, 0, z, 0, rows))
+        if stage == 2:
+            near = z ^ low
+            forwards = near & (near - 1) == 0
+            plan.append((1, near, low, 0, rows) if forwards else (1, 0, z, 0, rows))
+        plan.append((stage, z, side, 0, rows))
+        plan.append((stage, z, up, 0, rows))
+        if stage < 2:
+            plan.append((stage + 1, z ^ side, up, 0, middle))
+            plan.append((stage + 1, z ^ up, side, middle, rows))
+        else:
+            plan.append((stage, z, side ^ up, 0, rows))
+        plan.append((stage, z, core, 0, rows))
+        plan.append((stage + 1, z ^ side, core, 0, rows))
+        plan.append((stage + 1, z ^ up, core, 0, rows))
+        plan.append((min(stage + 2, 3), z ^ side ^ up, core, 0, rows))
+    return sorted(plan, key=lambda e: (e[0], e[2] == core))
+
+
 def kernel(
     n_row,
     n_ch,
+    plan,
     *refs,
 ):
     inputs, rest = refs[:11], refs[11:]
-    update_ref, gpair_ref, gwin_out, gwout_out = rest[:4]
+    update_ref, gpair_ref, gwin_ref, gwout_ref = rest[:4]
     held, rest = rest[4:15], rest[15:]
     (
         pair_ref,
@@ -79,7 +110,6 @@
         cot_ref,
     ) = held
     (
-        recv6, recv8, recv11,
         send1,
         recv1,
         send2,
@@ -90,19 +120,16 @@
         recv4,
         send5,
         recv5,
-        send6,
-        send7,
-        recv7,
-        send8,
-        send9,
-        recv9,
-        send10,
-        recv10,
-        send11,
+        early,
+        late,
+        blocks,
+        weights_t,
+        bias_t,
         send_sems,
         recv_sems,
+        plan_send,
+        plan_recv,
         load_sems,
-        store_sems,
     ) = rest
     n = n_row * n_ch
     rows, length, channels = pair_ref.shape
@@ -112,7 +139,6 @@
     my_row = lax.axis_index("row")
     my_ch = lax.axis_index("ch")
     me = my_row * n_ch + my_ch
-
     peers = farthest_first(n, n_ch)
 
     def place_of(t):
@@ -129,27 +155,84 @@
     for k in (0, 2, 3, 4, 5, 1, 10, 6, 7, 8, 9):
         loads[k].start()
 
-    def exchange(phase, src, dst, spread):
+    def exchange(phase, src, dst):
         for t in peers:
             d, place = place_of(t)
             pltpu.make_async_remote_copy(
-                src_ref=src.at[d] if spread else src,
+                src_ref=src.at[d],
                 dst_ref=dst.at[me],
                 send_sem=send_sems.at[phase],
                 recv_sem=recv_sems.at[phase],
                 device_id=place,
                 device_id_type=MESH,
             ).start()
-        if spread:
-            dst[me] = src[me]
+        dst[me] = src[me]
+
+    def wait_for(sems, phase, ref):
+        pltpu.make_async_copy(ref, ref, sems.at[phase]).wait()
 
     def arrived(phase, dst):
-        part = dst.at[pl.ds(0, n - 1)]
-        pltpu.make_async_copy(part, part, recv_sems.at[phase]).wait()
+        wait_for(recv_sems, phase, dst.at[pl.ds(0, n - 1)])
 
     def sent(phase, dst):
-        part = dst.at[pl.ds(0, n - 1)]
-        pltpu.make_async_copy(part, part, send_sems.at[phase]).wait()
+        wait_for(send_sems, phase, dst.at[pl.ds(0, n - 1)])
+
+    my_chip = me // 2
+    my_core = lax.rem(me, 2)
+
+    def spread(phase, ref):
+        for t in peers:
+            if t % 2 == 0:
+                mine = ref.at[my_chip, my_core]
+                pltpu.make_async_remote_copy(
+                    src_ref=mine,
+                    dst_ref=mine,
+                    send_sem=send_sems.at[phase],
+                    recv_sem=recv_sems.at[phase],
+                    device_id=place_of(t)[1],
+                    device_id_type=MESH,
+                ).start()
+
+    def same_core(ref):
+        return ref.at[pl.ds(0, n // 2 - 1), 0]
+
+    def hand_over(phase, ref):
+        mine = ref.at[:, my_core]
+        pltpu.make_async_remote_copy(
+            src_ref=mine,
+            dst_ref=mine,
+            send_sem=send_sems.at[phase],
+            recv_sem=recv_sems.at[phase],
+            device_id=place_of(1)[1],
+            device_id_type=MESH,
+        ).start()
+
+    def part_of(held_by, first, last):
+        return blocks.at[me ^ held_by, pl.ds(first, last - first)]
+
+    here = {0}
+
+    def ensure(block):
+        if block in here:
+            return
+        here.add(block)
+        for slot, (_, source, to, first, last) in enumerate(plan):
+            if source ^ to == block:
+                wait_for(plan_recv, slot, part_of(block, first, last))
+
+    def gather(stage):
+        for slot, (when, source, to, first, last) in enumerate(plan):
+            if when == stage:
+                ensure(source)
+                part = part_of(source, first, last)
+                pltpu.make_async_remote_copy(
+                    src_ref=part,
+                    dst_ref=part,
+                    send_sem=plan_send.at[slot],
+                    recv_sem=plan_recv.at[slot],
+                    device_id=place_of(to)[1],
+                    device_id_type=MESH,
+                ).start()
 
     def load_cells(ref):
         return jnp.concatenate(
@@ -208,8 +291,19 @@
     right = keep_tall * p3 * p4
     send1[:, :own, :] = split_h(left)
     send1[:, own:, :] = split_h(right)
+    blocks[me, :cells, :] = normed
+    for q in range(8):
+        at = min(q, cells // channels - 1) * channels
+        blocks[me, cells + q : cells + q + 1, :] = keep[:, at : at + channels]
     pl.semaphore_wait(barrier, n - 1)
-    exchange(0, send1, recv1, True)
+    exchange(0, send1, recv1)
+    gather(0)
+
+    for q, k in enumerate((0, 2)):
+        at = k * hidden
+        weights_t[q] = win_ref[:, at : at + hidden].T.reshape(n, own, channels)
+        column = b_ref[at // lanes : at // lanes + 1]
+        bias_t[q] = jnp.broadcast_to(column, (lanes, hidden)).T.reshape(n, own, lanes)
 
     gate = jax.nn.sigmoid(dot(normed, win_ref[:, width:], NN) + bias(width // lanes, b_ref.shape[0]))
     for k in range(6, 11):
@@ -221,7 +315,8 @@
     rights = [stack(recv1[:, own + h, :]) for h in range(own)]
     for h in range(own):
         send2[:, h, :] = unstack(dot(lefts[h], rights[h], NT))
-    exchange(1, send2, recv2, True)
+    exchange(1, send2, recv2)
+    gather(1)
     arrived(1, recv2)
 
     prod_hat, prod_scale = normalise(merge_h(recv2[...]))
@@ -232,86 +327,101 @@
         prod_hat, prod_scale, dot(d_out, wout_ref[...], NT) * gout_ref[...]
     )
     send3[...] = split_h(d_product)
-    exchange(2, send3, recv3, True)
+    exchange(2, send3, recv3)
 
     store_cells(update_ref, gate * projected)
     d_gate = cot * projected * gate * (1.0 - gate)
     d_wout = dot(normed_product, d_out, TN)
     d_wgate = dot(normed, d_gate, TN)
-    send4[...] = jnp.concatenate([d_wgate, d_wout], 1).reshape(n, own, channels + channels)
-    exchange(3, send4, recv4, True)
+    send4[:, :own, :] = d_wgate.reshape(n, own, channels)
+    send4[:, own:, :] = d_wout.reshape(n, own, channels)
+    exchange(3, send4, recv4)
+    gather(2)
     d_normed = dot(d_gate, win_ref[:, width:], NT)
 
     arrived(2, recv3)
     d_cols = [stack(recv3[:, h, :]) for h in range(own)]
     for h in range(own):
         send5[:, h, :] = unstack(dot(d_cols[h], rights[h], NN))
-    exchange(4, send5, recv5, True)
     for h in range(own):
-        send9[:, h, :] = unstack(dot(d_cols[h], lefts[h], TN))
-    exchange(8, send9, recv9, True)
+        send5[:, own + h, :] = unstack(dot(d_cols[h], lefts[h], TN))
+    exchange(4, send5, recv5)
+    gather(3)
 
     arrived(3, recv4)
-    send6[...] = jnp.sum(recv4[...], 0) / length
-    recv6[me] = send6[...]
-    exchange(5, send6, recv6, False)
+    early[my_chip, my_core] = jnp.sum(recv4[...], 0) / length
+    spread(5, early)
+    for block in range(1, n):
+        ensure(block)
+
+    group = 8
+    gate_weights = halves(jnp.concatenate([weights_t[0, me], weights_t[1, me]], 0))
+    gate_bias = jnp.concatenate([bias_t[0, me], bias_t[1, me]], 0)[:, :1]
+
+    def side_by_side(take, first):
+        return jnp.concatenate([take(first + i) for i in range(group)], 1)
+
+    def keep_of(d):
+        return jnp.concatenate(
+            [blocks[d, cells + q : cells + q + 1, :] for q in range(cells // channels)], 1
+        )
+
+    def grads_of(g, total):
+        first = g * group
+        x = jnp.concatenate([blocks[first + i, :cells, :] for i in range(group)], 0)
+        x = halves(x)
+        gates = jax.nn.sigmoid(dot_halves(gate_weights, x, NT) + gate_bias)
+        values = side_by_side(lambda d: recv1[d], first)
+        grads = side_by_side(lambda d: send5[d], first)
+        present = side_by_side(keep_of, first)
+        both = jnp.concatenate([grads * values * (1.0 - gates), grads * present * gates], 0)
+        return total + dot_halves(halves(both), x, NN)
+
+    total = lax.fori_loop(
+        0, n // group, grads_of, jnp.zeros((4 * own, channels), jnp.float32)
+    )
+    late[my_chip, my_core] = total / length
+    spread(6, late)
 
     arrived(4, recv5)
     half = 2 * hidden
-    d_left = merge_h(recv5[...]) * keep_tall
+    d_left = merge_h(recv5[:, :own, :]) * keep_tall
     d_first = jnp.concatenate([d_left * p2 * p1 * (1.0 - p1), d_left * p1], 1)
-    send7[...] = dot(normed, d_first, TN).reshape(n, own, half)
-    exchange(6, send7, recv7, True)
     d_normed = d_normed + dot(d_first, win_ref[:, :half], NT)
-    arrived(8, recv9)
-    d_right = merge_h(recv9[...]) * keep_tall
+    d_right = merge_h(recv5[:, own:, :]) * keep_tall
     d_second = jnp.concatenate([d_right * p4 * p3 * (1.0 - p3), d_right * p3], 1)
-    send10[...] = dot(normed, d_second, TN).reshape(n, own, half)
-    exchange(9, send10, recv10, True)
     d_normed = d_normed + dot(d_second, win_ref[:, half:width], NT)
     store_cells(gpair_ref, normalise_back(pair_hat, pair_scale, d_normed * gin_ref[...]))
-    arrived(6, recv7)
-    send8[...] = jnp.sum(recv7[...], 0) / length
-    exchange(7, send8, recv8, False)
-    recv8[me] = send8[...]
-    arrived(9, recv10)
-    send11[...] = jnp.sum(recv10[...], 0) / length
-    exchange(10, send11, recv11, False)
-    recv11[me] = send11[...]
-
-    arrived(5, recv6)
-    arrived(7, recv8)
-    arrived(10, recv11)
-    finish(None, None, recv6, recv8, recv11, None, None, gwin_out, gwout_out)
-    sent(0, recv1)
-    sent(1, recv2)
-    sent(2, recv3)
-    sent(3, recv4)
-    sent(4, recv5)
-    sent(5, recv6)
-    sent(6, recv7)
-    sent(7, recv8)
-    sent(8, recv9)
-    sent(9, recv10)
-    sent(10, recv11)
-
-
-def write_out(a, b, c, d, ao, bo, co, do, sems):
-    cs = [pltpu.make_async_copy(x, y, sems.at[k]) for k, (x, y) in enumerate(((a, ao), (b, bo), (c, co), (d, do)))]
-    for x in cs:
-        x.start()
-    for x in cs:
-        x.wait()
-
-
-def finish(update, gpair, early, late, last, update_ref, gpair_ref, gwin_ref, gwout_ref):
-    channels = gwin_ref.shape[0]
-    width = late.shape[2]
-    early_rows = early[...].reshape(channels, 2 * channels)
-    gwin_ref[:, 2 * width :] = early_rows[:, :channels]
-    gwout_ref[...] = early_rows[:, channels:]
-    gwin_ref[:, :width] = late[...].reshape(channels, width)
-    gwin_ref[:, width : 2 * width] = last[...].reshape(channels, width)
+
+    wait_for(recv_sems, 5, same_core(early))
+    hand_over(7, early)
+    wait_for(recv_sems, 6, same_core(late))
+    hand_over(8, late)
+    wait_for(recv_sems, 7, early.at[:, 0])
+    gwin_ref[:, width:] = early[:, :, :own, :].reshape(channels, channels)
+    gwout_ref[...] = early[:, :, own:, :].reshape(hidden, channels)
+    wait_for(recv_sems, 8, late.at[:, 0])
+    for q, k in enumerate((0, 2, 1, 3)):
+        piece = late[:, :, q * own : (q + 1) * own, :].reshape(hidden, channels)
+        gwin_ref[:, k * hidden : (k + 1) * hidden] = piece.T
+
+    for phase, ref in enumerate((recv1, recv2, recv3, recv4, recv5)):
+        sent(phase, ref)
+    for phase, ref in ((5, early), (6, late)):
+        wait_for(send_sems, phase, same_core(ref))
+    for phase, ref in ((7, early), (8, late)):
+        wait_for(send_sems, phase, ref.at[:, 0])
+    for slot, (_, source, _, first, last) in enumerate(plan):
+        wait_for(plan_send, slot, part_of(source, first, last))
+
+
+def write_out(a, b, c, d, a_out, b_out, c_out, d_out, sems):
+    pairs = ((a, a_out), (b, b_out), (c, c_out), (d, d_out))
+    copies = [pltpu.make_async_copy(x, y, sems.at[k]) for k, (x, y) in enumerate(pairs)]
+    for copy in copies:
+        copy.start()
+    for copy in copies:
+        copy.wait()
 
 
 def on_device(
@@ -352,45 +462,45 @@
         b_out[None],
         cotangent,
     )
+    lanes = min(128, hidden)
+    plan = gather_plan(n, n_ch, cells + 8)
     anywhere = pl.BlockSpec(memory_space=pl.ANY)
+    vmem = pl.BlockSpec(memory_space=pltpu.VMEM)
     inputs = tuple(pltpu.with_memory_space_constraint(x, pltpu.MemorySpace.HBM) for x in inputs)
+    out_shape = tuple(
+        jax.ShapeDtypeStruct(x.shape, f32) for x in (pair_rep, pair_rep, w_in, w_out)
+    )
     parts = pl.pallas_call(
-        functools.partial(kernel, n_row, n_ch),
-        out_shape=(
-            jax.ShapeDtypeStruct(pair_rep.shape, f32),
-            jax.ShapeDtypeStruct(pair_rep.shape, f32),
-            jax.ShapeDtypeStruct(w_in.shape, f32),
-            jax.ShapeDtypeStruct(w_out.shape, f32),
-        ),
+        functools.partial(kernel, n_row, n_ch, plan),
+        out_shape=out_shape,
         in_specs=[anywhere] * 11,
-        out_specs=(pl.BlockSpec(memory_space=pltpu.VMEM),) * 4,
+        out_specs=(vmem,) * 4,
         scratch_shapes=[
             *[pltpu.VMEM(x.shape, x.dtype) for x in inputs],
-            pltpu.VMEM((n, own, 2 * channels), f32),
-            pltpu.VMEM((n, own, 2 * hidden), f32),
-            pltpu.VMEM((n, own, 2 * hidden), f32),
             *both(2 * own, cells),
             *both(own, cells),
             *both(own, cells),
-            *both(own, 2 * channels),
-            *both(own, cells),
-            pltpu.VMEM((own, 2 * channels), f32),
-            *both(own, 2 * hidden),
-            pltpu.VMEM((own, 2 * hidden), f32),
-            *both(own, cells),
-            *both(own, 2 * hidden),
-            pltpu.VMEM((own, 2 * hidden), f32),
+            *both(2 * own, channels),
+            *both(2 * own, cells),
+            pltpu.VMEM((n // 2, 2, 2 * own, channels), f32),
+            pltpu.VMEM((n // 2, 2, 4 * own, channels), f32),
+            pltpu.VMEM((n, cells + 8, channels), f32),
+            pltpu.VMEM((2, n, own, channels), f32),
+            pltpu.VMEM((2, n, own, lanes), f32),
+            pltpu.SemaphoreType.DMA((9,)),
+            pltpu.SemaphoreType.DMA((9,)),
+            pltpu.SemaphoreType.DMA((len(plan),)),
+            pltpu.SemaphoreType.DMA((len(plan),)),
             pltpu.SemaphoreType.DMA((11,)),
-            pltpu.SemaphoreType.DMA((11,)),
-            pltpu.SemaphoreType.DMA((11,)),
-            pltpu.SemaphoreType.DMA((5,)),
         ],
-        compiler_params=pltpu.CompilerParams(collective_id=0, has_side_effects=True, vmem_limit_bytes=24 << 20),
+        compiler_params=pltpu.CompilerParams(
+            collective_id=0, has_side_effects=True, vmem_limit_bytes=56 << 20
+        ),
     )(*inputs)
     return pl.pallas_call(
         write_out,
-        out_shape=tuple(jax.ShapeDtypeStruct(x.shape, f32) for x in (pair_rep, pair_rep, w_in, w_out)),
-        in_specs=[pl.BlockSpec(memory_space=pltpu.VMEM)] * 4,
+        out_shape=out_shape,
+        in_specs=[vmem] * 4,
         out_specs=(anywhere,) * 4,
         scratch_shapes=[pltpu.SemaphoreType.DMA((4,))],
         compiler_params=pltpu.CompilerParams(vmem_limit_bytes=8 << 20),

time: 43.8 us -> 43.2 us (0.986)
  Pallas kernels: 43 us -> 38.7 us
  local copies, waits for them, and re-layouts: 0 us -> 3.48 us
    pallas_call x2, Pallas kernels: 43 us -> 38.7 us  [the longest x1 37.9 us: on_device(): pl.pallas_call(functools.partial(kernel, n_row, n_ch, plan), out_shape=ou...]
    unnamed x0 -> x8, local copies, waits for them, and re-layouts: none -> 3.48 us
where the time goes in v3:
time: 43.2 us; the launch traced here: 42.9 us
  Pallas kernels  38.7 us (90%)
  local copies, waits for them, and re-layouts  3.48 us (8%)
  between operations  0.65 us (2%)
    pallas_call x1, Pallas kernels, on_device(): pl.pallas_call(functools.partial(kernel, n_row, n_ch, plan), out_shape=ou...  37.9 us
    unnamed x8, local copies, waits for them, and re-layouts  3.48 us

profile of v3, /device:TPU:0, one launch (start us, length us, event | category | flops | bytes accessed | tf_op | source)
XLA Modules:
  0.0 42.9 jit_solution(16471749130965927116)
XLA Ops:
  0.6 37.9 %shard_map.138 = (f32[2,64,128]{2,1,0:T(8,128)}, f32[2,64,128]{2,1,0:T(8,128)}, f32[128,640]{1,0:T(8,128)}, f32[128,128]{1,0:T(8,128)}) custom-call(f32[2,64,128]{2,1,0:T(8,128)} %refs_0_.1, s32[2,64]{1,0:T(2,128)} %refs_1_.1, f32[1,128]{1,0:T(1,128)} %bitcast.7, f32[1,128]{1,0:T(1,128)} %bitcast.8, f32[128,640]{1,0:T(8,128)} %refs_4_.1, f32[5,128]{1,0:T(8,128)} %bitcast.6, ...), custom_call_target="tpu_custom_call" | custom-call | tf_op jit(solution)/shard_map/pallas_call | solution.py:473
  38.6 0.0 copy-start
  38.6 1.0 %copy-done = f32[128,640]{1,0:T(8,128)S(1)} copy-done((f32[128,640]{1,0:T(8,128)S(1)}, f32[128,640]{1,0:T(8,128)}, u32[]{:S(2)}) %copy-start) | copy-done | bytes 327704
  39.5 0.0 copy-start.1
  39.5 0.8 %copy-done.1 = f32[2,64,128]{2,1,0:T(8,128)S(1)} copy-done((f32[2,64,128]{2,1,0:T(8,128)S(1)}, f32[2,64,128]{2,1,0:T(8,128)}, u32[]{:S(2)}) %copy-start.1) | copy-done | bytes 65560
  40.4 0.0 copy-start.2
  40.4 0.8 %copy-done.2 = f32[2,64,128]{2,1,0:T(8,128)S(1)} copy-done((f32[2,64,128]{2,1,0:T(8,128)S(1)}, f32[2,64,128]{2,1,0:T(8,128)}, u32[]{:S(2)}) %copy-start.2) | copy-done | bytes 65560
  41.2 0.0 copy-start.3
  41.2 0.8 %copy-done.3 = f32[128,128]{1,0:T(8,128)S(1)} copy-done((f32[128,128]{1,0:T(8,128)S(1)}, f32[128,128]{1,0:T(8,128)}, u32[]{:S(2)}) %copy-start.3) | copy-done | bytes 65560
  42.0 0.8 %shard_map.139 = (f32[2,64,128]{2,1,0:T(8,128)}, f32[2,64,128]{2,1,0:T(8,128)}, f32[128,640]{1,0:T(8,128)}, f32[128,128]{1,0:T(8,128)}) custom-call(f32[2,64,128]{2,1,0:T(8,128)S(1)} %copy-done.1, f32[2,64,128]{2,1,0:T(8,128)S(1)} %copy-done.2, f32[128,640]{1,0:T(8,128)S(1)} %copy-done, f32[128,128]{1,0:T(8,128)S(1)} %copy-done.3), custom_call_target="tpu_custom_call" | custom-call | tf_op jit(solution)/shard_map/pallas_call | solution.py:500
Async XLA Ops:
  38.6 1.0 %copy-start = (f32[128,640]{1,0:T(8,128)S(1)}, f32[128,640]{1,0:T(8,128)}, u32[]{:S(2)}) copy-start(f32[128,640]{1,0:T(8,128)} %get-tuple-element.10.c) | copy-start | bytes 983044
  39.5 0.8 %copy-start.1 = (f32[2,64,128]{2,1,0:T(8,128)S(1)}, f32[2,64,128]{2,1,0:T(8,128)}, u32[]{:S(2)}) copy-start(f32[2,64,128]{2,1,0:T(8,128)} %get-tuple-element.8.a) | copy-start | bytes 196612
  40.4 0.8 %copy-start.2 = (f32[2,64,128]{2,1,0:T(8,128)S(1)}, f32[2,64,128]{2,1,0:T(8,128)}, u32[]{:S(2)}) copy-start(f32[2,64,128]{2,1,0:T(8,128)} %get-tuple-element.9.b) | copy-start | bytes 196612
  41.2 0.8 %copy-start.3 = (f32[128,128]{1,0:T(8,128)S(1)}, f32[128,128]{1,0:T(8,128)}, u32[]{:S(2)}) copy-start(f32[128,128]{1,0:T(8,128)} %get-tuple-element.11.d) | copy-start | bytes 196612

commit v4 on v3

--- a/solution.py
+++ b/solution.py
@@ -75,15 +75,17 @@
             plan.append((1, near, low, 0, rows) if forwards else (1, 0, z, 0, rows))
         plan.append((stage, z, side, 0, rows))
         plan.append((stage, z, up, 0, rows))
-        if stage < 2:
+        if stage == 0:
+            plan.append((0, 0, side ^ up, 0, rows))
+        elif stage < 2:
             plan.append((stage + 1, z ^ side, up, 0, middle))
             plan.append((stage + 1, z ^ up, side, middle, rows))
         else:
-            plan.append((stage, z, side ^ up, 0, rows))
+            plan.append((1, 0, z ^ side ^ up, 0, rows))
         plan.append((stage, z, core, 0, rows))
         plan.append((stage + 1, z ^ side, core, 0, rows))
         plan.append((stage + 1, z ^ up, core, 0, rows))
-        plan.append((min(stage + 2, 3), z ^ side ^ up, core, 0, rows))
+        plan.append((1 if z == 0 else min(stage + 2, 3), z ^ side ^ up, core, 0, rows))
     return sorted(plan, key=lambda e: (e[0], e[2] == core))
 
 
@@ -117,6 +119,8 @@
         send3,
         recv3,
         send4,
+        pair4,
+        sum4,
         recv4,
         send5,
         recv5,
@@ -155,17 +159,19 @@
     for k in (0, 2, 3, 4, 5, 1, 10, 6, 7, 8, 9):
         loads[k].start()
 
+    def remote(phase, src, dst, to):
+        pltpu.make_async_remote_copy(
+            src_ref=src,
+            dst_ref=dst,
+            send_sem=send_sems.at[phase],
+            recv_sem=recv_sems.at[phase],
+            device_id=place_of(to)[1],
+            device_id_type=MESH,
+        ).start()
+
     def exchange(phase, src, dst):
         for t in peers:
-            d, place = place_of(t)
-            pltpu.make_async_remote_copy(
-                src_ref=src.at[d],
-                dst_ref=dst.at[me],
-                send_sem=send_sems.at[phase],
-                recv_sem=recv_sems.at[phase],
-                device_id=place,
-                device_id_type=MESH,
-            ).start()
+            remote(phase, src.at[place_of(t)[0]], dst.at[me], t)
         dst[me] = src[me]
 
     def wait_for(sems, phase, ref):
@@ -184,28 +190,14 @@
         for t in peers:
             if t % 2 == 0:
                 mine = ref.at[my_chip, my_core]
-                pltpu.make_async_remote_copy(
-                    src_ref=mine,
-                    dst_ref=mine,
-                    send_sem=send_sems.at[phase],
-                    recv_sem=recv_sems.at[phase],
-                    device_id=place_of(t)[1],
-                    device_id_type=MESH,
-                ).start()
+                remote(phase, mine, mine, t)
 
     def same_core(ref):
         return ref.at[pl.ds(0, n // 2 - 1), 0]
 
     def hand_over(phase, ref):
         mine = ref.at[:, my_core]
-        pltpu.make_async_remote_copy(
-            src_ref=mine,
-            dst_ref=mine,
-            send_sem=send_sems.at[phase],
-            recv_sem=recv_sems.at[phase],
-            device_id=place_of(1)[1],
-            device_id_type=MESH,
-        ).start()
+        remote(phase, mine, mine, 1)
 
     def part_of(held_by, first, last):
         return blocks.at[me ^ held_by, pl.ds(first, last - first)]
@@ -333,11 +325,17 @@
     d_gate = cot * projected * gate * (1.0 - gate)
     d_wout = dot(normed_product, d_out, TN)
     d_wgate = dot(normed, d_gate, TN)
-    send4[:, :own, :] = d_wgate.reshape(n, own, channels)
-    send4[:, own:, :] = d_wout.reshape(n, own, channels)
-    exchange(3, send4, recv4)
+    send4[:, :, :own, :] = d_wgate.reshape(n // 2, 2, own, channels)
+    send4[:, :, own:, :] = d_wout.reshape(n // 2, 2, own, channels)
+    remote(9, send4.at[:, 1 - my_core], pair4, 1)
     gather(2)
     d_normed = dot(d_gate, win_ref[:, width:], NT)
+    wait_for(recv_sems, 9, pair4)
+    sum4[...] = send4[:, my_core] + pair4[...]
+    for t in peers:
+        if t % 2 == 0:
+            remote(3, sum4.at[place_of(t)[0] // 2], recv4.at[my_chip], t)
+    recv4[my_chip] = sum4[my_chip]
 
     arrived(2, recv3)
     d_cols = [stack(recv3[:, h, :]) for h in range(own)]
@@ -346,40 +344,44 @@
     for h in range(own):
         send5[:, own + h, :] = unstack(dot(d_cols[h], lefts[h], TN))
     exchange(4, send5, recv5)
-    gather(3)
-
-    arrived(3, recv4)
-    early[my_chip, my_core] = jnp.sum(recv4[...], 0) / length
-    spread(5, early)
-    for block in range(1, n):
-        ensure(block)
-
-    group = 8
+
     gate_weights = halves(jnp.concatenate([weights_t[0, me], weights_t[1, me]], 0))
     gate_bias = jnp.concatenate([bias_t[0, me], bias_t[1, me]], 0)[:, :1]
-
-    def side_by_side(take, first):
-        return jnp.concatenate([take(first + i) for i in range(group)], 1)
 
     def keep_of(d):
         return jnp.concatenate(
             [blocks[d, cells + q : cells + q + 1, :] for q in range(cells // channels)], 1
         )
 
-    def grads_of(g, total):
-        first = g * group
-        x = jnp.concatenate([blocks[first + i, :cells, :] for i in range(group)], 0)
-        x = halves(x)
+    def grads_of(offsets):
+        devices = [me ^ t for t in offsets]
+
+        def side_by_side(take):
+            return jnp.concatenate([take(d) for d in devices], 1)
+
+        x = halves(jnp.concatenate([blocks[d, :cells, :] for d in devices], 0))
         gates = jax.nn.sigmoid(dot_halves(gate_weights, x, NT) + gate_bias)
-        values = side_by_side(lambda d: recv1[d], first)
-        grads = side_by_side(lambda d: send5[d], first)
-        present = side_by_side(keep_of, first)
+        values = side_by_side(lambda d: recv1[d])
+        grads = side_by_side(lambda d: send5[d])
+        present = side_by_side(keep_of)
         both = jnp.concatenate([grads * values * (1.0 - gates), grads * present * gates], 0)
-        return total + dot_halves(halves(both), x, NN)
-
-    total = lax.fori_loop(
-        0, n // group, grads_of, jnp.zeros((4 * own, channels), jnp.float32)
-    )
+        return dot_halves(halves(both), x, NN)
+
+    def came_in(stage):
+        return sorted({e[1] ^ e[2] for e in plan if e[0] == stage})
+
+    first_ones = [0, *came_in(0), *came_in(1)]
+    for block in first_ones:
+        ensure(block)
+    total = grads_of(first_ones)
+    wait_for(recv_sems, 3, recv4.at[pl.ds(0, n // 2 - 1)])
+    early[my_chip, my_core] = jnp.sum(recv4[...], 0) / length
+    spread(5, early)
+    gather(3)
+    for stage in (2, 3):
+        for block in came_in(stage):
+            ensure(block)
+        total = total + grads_of(came_in(stage))
     late[my_chip, my_core] = total / length
     spread(6, late)
 
@@ -405,8 +407,10 @@
         piece = late[:, :, q * own : (q + 1) * own, :].reshape(hidden, channels)
         gwin_ref[:, k * hidden : (k + 1) * hidden] = piece.T
 
-    for phase, ref in enumerate((recv1, recv2, recv3, recv4, recv5)):
+    for phase, ref in ((0, recv1), (1, recv2), (2, recv3), (4, recv5)):
         sent(phase, ref)
+    wait_for(send_sems, 3, recv4.at[pl.ds(0, n // 2 - 1)])
+    wait_for(send_sems, 9, pair4)
     for phase, ref in ((5, early), (6, late)):
         wait_for(send_sems, phase, same_core(ref))
     for phase, ref in ((7, early), (8, late)):
@@ -480,15 +484,16 @@
             *both(2 * own, cells),
             *both(own, cells),
             *both(own, cells),
-            *both(2 * own, channels),
+            pltpu.VMEM((n // 2, 2, 2 * own, channels), f32),
+            *[pltpu.VMEM((n // 2, 2 * own, channels), f32)] * 3,
             *both(2 * own, cells),
             pltpu.VMEM((n // 2, 2, 2 * own, channels), f32),
             pltpu.VMEM((n // 2, 2, 4 * own, channels), f32),
             pltpu.VMEM((n, cells + 8, channels), f32),
             pltpu.VMEM((2, n, own, channels), f32),
             pltpu.VMEM((2, n, own, lanes), f32),
-            pltpu.SemaphoreType.DMA((9,)),
-            pltpu.SemaphoreType.DMA((9,)),
+            pltpu.SemaphoreType.DMA((10,)),
+            pltpu.SemaphoreType.DMA((10,)),
             pltpu.SemaphoreType.DMA((len(plan),)),
             pltpu.SemaphoreType.DMA((len(plan),)),
             pltpu.SemaphoreType.DMA((11,)),

time: 43.2 us -> 40 us (0.926)
  Pallas kernels: 38.7 us -> 35.6 us
    pallas_call x1, Pallas kernels: 37.9 us -> 34.8 us  [on_device(): pl.pallas_call(functools.partial(kernel, n_row, n_ch, plan), out_shape=ou...]
where the time goes in v4:
time: 40 us; the launch traced here: 39.7 us
  Pallas kernels  35.6 us (89%)
  local copies, waits for them, and re-layouts  3.48 us (9%)
  between operations  0.65 us (2%)
    pallas_call x1, Pallas kernels, on_device(): pl.pallas_call(functools.partial(kernel, n_row, n_ch, plan), out_shape=ou...  34.8 us
    unnamed x8, local copies, waits for them, and re-layouts  3.48 us
    pallas_call x1, Pallas kernels, on_device(): pl.pallas_call(write_out, out_shape=out_shape, in_specs=[vmem] * 4, out_s...  0.81 us

profile of v4, /device:TPU:0, one launch (start us, length us, event | category | flops | bytes accessed | tf_op | source)
XLA Modules:
  0.0 39.7 jit_solution(1118170085398395883)
XLA Ops:
  0.6 34.8 %shard_map.138 = (f32[2,64,128]{2,1,0:T(8,128)}, f32[2,64,128]{2,1,0:T(8,128)}, f32[128,640]{1,0:T(8,128)}, f32[128,128]{1,0:T(8,128)}) custom-call(f32[2,64,128]{2,1,0:T(8,128)} %refs_0_.1, s32[2,64]{1,0:T(2,128)} %refs_1_.1, f32[1,128]{1,0:T(1,128)} %bitcast.7, f32[1,128]{1,0:T(1,128)} %bitcast.8, f32[128,640]{1,0:T(8,128)} %refs_4_.1, f32[5,128]{1,0:T(8,128)} %bitcast.6, ...), custom_call_target="tpu_custom_call" | custom-call | tf_op jit(solution)/shard_map/pallas_call | solution.py:477
  35.4 0.0 copy-start
  35.4 1.0 %copy-done = f32[128,640]{1,0:T(8,128)S(1)} copy-done((f32[128,640]{1,0:T(8,128)S(1)}, f32[128,640]{1,0:T(8,128)}, u32[]{:S(2)}) %copy-start) | copy-done | bytes 327704
  36.4 0.0 copy-start.1
  36.4 0.8 %copy-done.1 = f32[2,64,128]{2,1,0:T(8,128)S(1)} copy-done((f32[2,64,128]{2,1,0:T(8,128)S(1)}, f32[2,64,128]{2,1,0:T(8,128)}, u32[]{:S(2)}) %copy-start.1) | copy-done | bytes 65560
  37.2 0.0 copy-start.2
  37.2 0.8 %copy-done.2 = f32[2,64,128]{2,1,0:T(8,128)S(1)} copy-done((f32[2,64,128]{2,1,0:T(8,128)S(1)}, f32[2,64,128]{2,1,0:T(8,128)}, u32[]{:S(2)}) %copy-start.2) | copy-done | bytes 65560
  38.1 0.0 copy-start.3
  38.1 0.8 %copy-done.3 = f32[128,128]{1,0:T(8,128)S(1)} copy-done((f32[128,128]{1,0:T(8,128)S(1)}, f32[128,128]{1,0:T(8,128)}, u32[]{:S(2)}) %copy-start.3) | copy-done | bytes 65560
  38.9 0.8 %shard_map.139 = (f32[2,64,128]{2,1,0:T(8,128)}, f32[2,64,128]{2,1,0:T(8,128)}, f32[128,640]{1,0:T(8,128)}, f32[128,128]{1,0:T(8,128)}) custom-call(f32[2,64,128]{2,1,0:T(8,128)S(1)} %copy-done.1, f32[2,64,128]{2,1,0:T(8,128)S(1)} %copy-done.2, f32[128,640]{1,0:T(8,128)S(1)} %copy-done, f32[128,128]{1,0:T(8,128)S(1)} %copy-done.3), custom_call_target="tpu_custom_call" | custom-call | tf_op jit(solution)/shard_map/pallas_call | solution.py:505
Async XLA Ops:
  35.4 1.0 %copy-start = (f32[128,640]{1,0:T(8,128)S(1)}, f32[128,640]{1,0:T(8,128)}, u32[]{:S(2)}) copy-start(f32[128,640]{1,0:T(8,128)} %get-tuple-element.10.c) | copy-start | bytes 983044
  36.4 0.8 %copy-start.1 = (f32[2,64,128]{2,1,0:T(8,128)S(1)}, f32[2,64,128]{2,1,0:T(8,128)}, u32[]{:S(2)}) copy-start(f32[2,64,128]{2,1,0:T(8,128)} %get-tuple-element.8.a) | copy-start | bytes 196612
  37.2 0.8 %copy-start.2 = (f32[2,64,128]{2,1,0:T(8,128)S(1)}, f32[2,64,128]{2,1,0:T(8,128)}, u32[]{:S(2)}) copy-start(f32[2,64,128]{2,1,0:T(8,128)} %get-tuple-element.9.b) | copy-start | bytes 196612
  38.1 0.8 %copy-start.3 = (f32[128,128]{1,0:T(8,128)S(1)}, f32[128,128]{1,0:T(8,128)}, u32[]{:S(2)}) copy-start(f32[128,128]{1,0:T(8,128)} %get-tuple-element.11.d) | copy-start | bytes 196612

commit v5 on v4

--- a/solution.py
+++ b/solution.py
@@ -499,7 +499,9 @@
             pltpu.SemaphoreType.DMA((11,)),
         ],
         compiler_params=pltpu.CompilerParams(
-            collective_id=0, has_side_effects=True, vmem_limit_bytes=56 << 20
+            collective_id=0,
+            has_side_effects=True,
+            vmem_limit_bytes=n * (cells + 8) * channels * 4 + (22 << 20),
         ),
     )(*inputs)
     return pl.pallas_call(

time: 40 us -> 35.6 us (0.89)
  local copies, waits for them, and re-layouts: 3.48 us -> 0 us
  Pallas kernels: 35.6 us -> 34.8 us
    unnamed x8 -> x0, local copies, waits for them, and re-layouts: 3.48 us -> none
    pallas_call x1, Pallas kernels: 34.8 us -> 34 us  [on_device(): pl.pallas_call(functools.partial(kernel, n_row, n_ch, plan), out_shape=ou...]
where the time goes in v5:
time: 35.6 us; the launch traced here: 35.4 us
  Pallas kernels  34.8 us (98%)
  between operations  0.64 us (2%)
    pallas_call x1, Pallas kernels, on_device(): pl.pallas_call(functools.partial(kernel, n_row, n_ch, plan), out_shape=ou...  34 us
    pallas_call x1, Pallas kernels, on_device(): pl.pallas_call(write_out, out_shape=out_shape, in_specs=[vmem] * 4, out_s...  0.82 us

profile of v5, /device:TPU:0, one launch (start us, length us, event | category | flops | bytes accessed | tf_op | source)
XLA Modules:
  0.0 35.4 jit_solution(13056078535581360396)
XLA Ops:
  0.6 34.0 %shard_map.138 = (f32[2,64,128]{2,1,0:T(8,128)S(1)}, f32[2,64,128]{2,1,0:T(8,128)S(1)}, f32[128,640]{1,0:T(8,128)S(1)}, f32[128,128]{1,0:T(8,128)S(1)}) custom-call(f32[2,64,128]{2,1,0:T(8,128)} %refs_0_.1, s32[2,64]{1,0:T(2,128)} %refs_1_.1, f32[1,128]{1,0:T(1,128)} %bitcast.7, f32[1,128]{1,0:T(1,128)} %bitcast.8, f32[128,640]{1,0:T(8,128)} %refs_4_.1, ...), custom_call_target="tpu_custom_call" | custom-call | tf_op jit(solution)/shard_map/pallas_call | solution.py:477
  34.6 0.8 %shard_map.139 = (f32[2,64,128]{2,1,0:T(8,128)}, f32[2,64,128]{2,1,0:T(8,128)}, f32[128,640]{1,0:T(8,128)}, f32[128,128]{1,0:T(8,128)}) custom-call(f32[2,64,128]{2,1,0:T(8,128)S(1)} %get-tuple-element.8.a, f32[2,64,128]{2,1,0:T(8,128)S(1)} %get-tuple-element.9.b, f32[128,640]{1,0:T(8,128)S(1)} %get-tuple-element.10.c, f32[128,128]{1,0:T(8,128)S(1)} %get-tuple-element.11.d), custom_call_target="tpu_custom_call" | custom-call | tf_op jit(solution)/shard_map/pallas_call | solution.py:507

commit v6 on v5

--- a/solution.py
+++ b/solution.py
@@ -81,12 +81,12 @@
             plan.append((stage + 1, z ^ side, up, 0, middle))
             plan.append((stage + 1, z ^ up, side, middle, rows))
         else:
-            plan.append((1, 0, z ^ side ^ up, 0, rows))
+            plan.append((1, side ^ up, z, 0, rows))
         plan.append((stage, z, core, 0, rows))
         plan.append((stage + 1, z ^ side, core, 0, rows))
         plan.append((stage + 1, z ^ up, core, 0, rows))
         plan.append((1 if z == 0 else min(stage + 2, 3), z ^ side ^ up, core, 0, rows))
-    return sorted(plan, key=lambda e: (e[0], e[2] == core))
+    return sorted(plan, key=lambda e: (e[0], e[2] == core, e[1] > 2 * n_ch and e[2] < 2 * n_ch))
 
 
 def kernel(
@@ -126,6 +126,7 @@
         recv5,
         early,
         late,
+        factors,
         blocks,
         weights_t,
         bias_t,
@@ -320,6 +321,7 @@
     )
     send3[...] = split_h(d_product)
     exchange(2, send3, recv3)
+    gather(2)
 
     store_cells(update_ref, gate * projected)
     d_gate = cot * projected * gate * (1.0 - gate)
@@ -327,15 +329,48 @@
     d_wgate = dot(normed, d_gate, TN)
     send4[:, :, :own, :] = d_wgate.reshape(n // 2, 2, own, channels)
     send4[:, :, own:, :] = d_wout.reshape(n // 2, 2, own, channels)
-    remote(9, send4.at[:, 1 - my_core], pair4, 1)
-    gather(2)
+    remote(7, send4.at[:, 1 - my_core], pair4, 1)
     d_normed = dot(d_gate, win_ref[:, width:], NT)
-    wait_for(recv_sems, 9, pair4)
+    wait_for(recv_sems, 7, pair4)
     sum4[...] = send4[:, my_core] + pair4[...]
     for t in peers:
         if t % 2 == 0:
             remote(3, sum4.at[place_of(t)[0] // 2], recv4.at[my_chip], t)
     recv4[my_chip] = sum4[my_chip]
+
+    gate_weights = halves(jnp.concatenate([weights_t[0, me], weights_t[1, me]], 0))
+    gate_bias = jnp.concatenate([bias_t[0, me], bias_t[1, me]], 0)[:, :1]
+
+    def keep_of(d):
+        return jnp.concatenate(
+            [blocks[d, cells + q : cells + q + 1, :] for q in range(cells // channels)], 1
+        )
+
+    def side_by_side(take, offsets):
+        return jnp.concatenate([take(me ^ t) for t in offsets], 1)
+
+    def block_halves(offsets):
+        return halves(jnp.concatenate([blocks[me ^ t, :cells, :] for t in offsets], 0))
+
+    def factors_of(offsets, x):
+        gates = jax.nn.sigmoid(dot_halves(gate_weights, x, NT) + gate_bias)
+        values = side_by_side(lambda d: recv1[d], offsets)
+        present = side_by_side(keep_of, offsets)
+        return jnp.concatenate([values * (1.0 - gates), present * gates], 0)
+
+    def grads_of(offsets, x, scaled):
+        grads = side_by_side(lambda d: send5[d], offsets)
+        return dot_halves(halves(jnp.concatenate([grads, grads], 0) * scaled), x, NN)
+
+    def came_in(stage):
+        return sorted({e[1] ^ e[2] for e in plan if e[0] == stage})
+
+    first_ones = [0, *came_in(0), *came_in(1)]
+    for block in first_ones:
+        ensure(block)
+    first_factors = factors_of(first_ones, block_halves(first_ones))
+    for at, t in enumerate(first_ones):
+        factors[me ^ t] = first_factors[:, at * cells : (at + 1) * cells]
 
     arrived(2, recv3)
     d_cols = [stack(recv3[:, h, :]) for h in range(own)]
@@ -344,46 +379,20 @@
     for h in range(own):
         send5[:, own + h, :] = unstack(dot(d_cols[h], lefts[h], TN))
     exchange(4, send5, recv5)
-
-    gate_weights = halves(jnp.concatenate([weights_t[0, me], weights_t[1, me]], 0))
-    gate_bias = jnp.concatenate([bias_t[0, me], bias_t[1, me]], 0)[:, :1]
-
-    def keep_of(d):
-        return jnp.concatenate(
-            [blocks[d, cells + q : cells + q + 1, :] for q in range(cells // channels)], 1
-        )
-
-    def grads_of(offsets):
-        devices = [me ^ t for t in offsets]
-
-        def side_by_side(take):
-            return jnp.concatenate([take(d) for d in devices], 1)
-
-        x = halves(jnp.concatenate([blocks[d, :cells, :] for d in devices], 0))
-        gates = jax.nn.sigmoid(dot_halves(gate_weights, x, NT) + gate_bias)
-        values = side_by_side(lambda d: recv1[d])
-        grads = side_by_side(lambda d: send5[d])
-        present = side_by_side(keep_of)
-        both = jnp.concatenate([grads * values * (1.0 - gates), grads * present * gates], 0)
-        return dot_halves(halves(both), x, NN)
-
-    def came_in(stage):
-        return sorted({e[1] ^ e[2] for e in plan if e[0] == stage})
-
-    first_ones = [0, *came_in(0), *came_in(1)]
-    for block in first_ones:
-        ensure(block)
-    total = grads_of(first_ones)
+    gather(3)
+    total = grads_of(
+        first_ones, block_halves(first_ones), side_by_side(lambda d: factors[d], first_ones)
+    )
     wait_for(recv_sems, 3, recv4.at[pl.ds(0, n // 2 - 1)])
     early[my_chip, my_core] = jnp.sum(recv4[...], 0) / length
-    spread(5, early)
-    gather(3)
+    spread(8, early)
     for stage in (2, 3):
         for block in came_in(stage):
             ensure(block)
-        total = total + grads_of(came_in(stage))
+        x = block_halves(came_in(stage))
+        total = total + grads_of(came_in(stage), x, factors_of(came_in(stage), x))
     late[my_chip, my_core] = total / length
-    spread(6, late)
+    spread(5, late)
 
     arrived(4, recv5)
     half = 2 * hidden
@@ -395,28 +404,28 @@
     d_normed = d_normed + dot(d_second, win_ref[:, half:width], NT)
     store_cells(gpair_ref, normalise_back(pair_hat, pair_scale, d_normed * gin_ref[...]))
 
-    wait_for(recv_sems, 5, same_core(early))
-    hand_over(7, early)
-    wait_for(recv_sems, 6, same_core(late))
-    hand_over(8, late)
-    wait_for(recv_sems, 7, early.at[:, 0])
+    wait_for(recv_sems, 8, same_core(early))
+    hand_over(9, early)
+    for phase, ref in ((0, recv1), (1, recv2), (2, recv3), (4, recv5)):
+        sent(phase, ref)
+    wait_for(send_sems, 3, recv4.at[pl.ds(0, n // 2 - 1)])
+    wait_for(send_sems, 7, pair4)
+    for slot, (_, source, _, first, last) in enumerate(plan):
+        wait_for(plan_send, slot, part_of(source, first, last))
+    wait_for(send_sems, 8, same_core(early))
+    wait_for(recv_sems, 5, same_core(late))
+    hand_over(6, late)
+    wait_for(recv_sems, 9, early.at[:, 0])
     gwin_ref[:, width:] = early[:, :, :own, :].reshape(channels, channels)
     gwout_ref[...] = early[:, :, own:, :].reshape(hidden, channels)
-    wait_for(recv_sems, 8, late.at[:, 0])
+    wait_for(recv_sems, 6, late.at[:, 0])
     for q, k in enumerate((0, 2, 1, 3)):
         piece = late[:, :, q * own : (q + 1) * own, :].reshape(hidden, channels)
         gwin_ref[:, k * hidden : (k + 1) * hidden] = piece.T
 
-    for phase, ref in ((0, recv1), (1, recv2), (2, recv3), (4, recv5)):
-        sent(phase, ref)
-    wait_for(send_sems, 3, recv4.at[pl.ds(0, n // 2 - 1)])
-    wait_for(send_sems, 9, pair4)
-    for phase, ref in ((5, early), (6, late)):
-        wait_for(send_sems, phase, same_core(ref))
-    for phase, ref in ((7, early), (8, late)):
+    wait_for(send_sems, 5, same_core(late))
+    for phase, ref in ((9, early), (6, late)):
         wait_for(send_sems, phase, ref.at[:, 0])
-    for slot, (_, source, _, first, last) in enumerate(plan):
-        wait_for(plan_send, slot, part_of(source, first, last))
 
 
 def write_out(a, b, c, d, a_out, b_out, c_out, d_out, sems):
@@ -489,6 +498,7 @@
             *both(2 * own, cells),
             pltpu.VMEM((n // 2, 2, 2 * own, channels), f32),
             pltpu.VMEM((n // 2, 2, 4 * own, channels), f32),
+            pltpu.VMEM((n, 4 * own, cells), f32),
             pltpu.VMEM((n, cells + 8, channels), f32),
             pltpu.VMEM((2, n, own, channels), f32),
             pltpu.VMEM((2, n, own, lanes), f32),

time: 35.6 us -> 35.2 us (0.989)
  Pallas kernels: 34.8 us -> 34.4 us
    pallas_call x1, Pallas kernels: 34 us -> 33.6 us  [on_device(): pl.pallas_call(functools.partial(kernel, n_row, n_ch, plan), out_shape=ou...]
where the time goes in v6:
time: 35.2 us; the launch traced here: 35 us
  Pallas kernels  34.4 us (98%)
  between operations  0.64 us (2%)
    pallas_call x1, Pallas kernels, on_device(): pl.pallas_call(functools.partial(kernel, n_row, n_ch, plan), out_shape=ou...  33.6 us
    pallas_call x1, Pallas kernels, on_device(): pl.pallas_call(write_out, out_shape=out_shape, in_specs=[vmem] * 4, out_s...  0.82 us

profile of v6, /device:TPU:0, one launch (start us, length us, event | category | flops | bytes accessed | tf_op | source)
XLA Modules:
  0.0 35.0 jit_solution(16498235933360885901)
XLA Ops:
  0.6 33.6 %shard_map.138 = (f32[2,64,128]{2,1,0:T(8,128)S(1)}, f32[2,64,128]{2,1,0:T(8,128)S(1)}, f32[128,640]{1,0:T(8,128)S(1)}, f32[128,128]{1,0:T(8,128)S(1)}) custom-call(f32[2,64,128]{2,1,0:T(8,128)} %refs_0_.1, s32[2,64]{1,0:T(2,128)} %refs_1_.1, f32[1,128]{1,0:T(1,128)} %bitcast.7, f32[1,128]{1,0:T(1,128)} %bitcast.8, f32[128,640]{1,0:T(8,128)} %refs_4_.1, ...), custom_call_target="tpu_custom_call" | custom-call | tf_op jit(solution)/shard_map/pallas_call | solution.py:486
  34.2 0.8 %shard_map.139 = (f32[2,64,128]{2,1,0:T(8,128)}, f32[2,64,128]{2,1,0:T(8,128)}, f32[128,640]{1,0:T(8,128)}, f32[128,128]{1,0:T(8,128)}) custom-call(f32[2,64,128]{2,1,0:T(8,128)S(1)} %get-tuple-element.8.a, f32[2,64,128]{2,1,0:T(8,128)S(1)} %get-tuple-element.9.b, f32[128,640]{1,0:T(8,128)S(1)} %get-tuple-element.10.c, f32[128,128]{1,0:T(8,128)S(1)} %get-tuple-element.11.d), custom_call_target="tpu_custom_call" | custom-call | tf_op jit(solution)/shard_map/pallas_call | solution.py:517

commit v7 on v6

--- a/solution.py
+++ b/solution.py
@@ -57,7 +57,7 @@
         row, ch = divmod(t, n_ch)
         return (row // 2).bit_length() + row % 2 + ch // 2
 
-    return sorted(range(1, n), key=lambda t: (hops(t), t), reverse=True)
+    return sorted(range(1, n), key=lambda t: (-hops(t), t % 2, t))
 
 
 def gather_plan(n, n_ch, rows):

time: 35.2 us -> 34.5 us (0.980)
  Pallas kernels: 34.4 us -> 33.7 us
    pallas_call x1, Pallas kernels: 33.6 us -> 32.9 us  [on_device(): pl.pallas_call(functools.partial(kernel, n_row, n_ch, plan), out_shape=ou...]
where the time goes in v7:
time: 34.5 us; the launch traced here: 34.3 us
  Pallas kernels  33.7 us (98%)
  between operations  0.64 us (2%)
    pallas_call x1, Pallas kernels, on_device(): pl.pallas_call(functools.partial(kernel, n_row, n_ch, plan), out_shape=ou...  32.9 us
    pallas_call x1, Pallas kernels, on_device(): pl.pallas_call(write_out, out_shape=out_shape, in_specs=[vmem] * 4, out_s...  0.82 us

profile of v7, /device:TPU:0, one launch (start us, length us, event | category | flops | bytes accessed | tf_op | source)
XLA Modules:
  0.0 34.3 jit_solution(3572244663104601743)
XLA Ops:
  0.6 32.9 %shard_map.138 = (f32[2,64,128]{2,1,0:T(8,128)S(1)}, f32[2,64,128]{2,1,0:T(8,128)S(1)}, f32[128,640]{1,0:T(8,128)S(1)}, f32[128,128]{1,0:T(8,128)S(1)}) custom-call(f32[2,64,128]{2,1,0:T(8,128)} %refs_0_.1, s32[2,64]{1,0:T(2,128)} %refs_1_.1, f32[1,128]{1,0:T(1,128)} %bitcast.7, f32[1,128]{1,0:T(1,128)} %bitcast.8, f32[128,640]{1,0:T(8,128)} %refs_4_.1, ...), custom_call_target="tpu_custom_call" | custom-call | tf_op jit(solution)/shard_map/pallas_call | solution.py:486
  33.5 0.8 %shard_map.139 = (f32[2,64,128]{2,1,0:T(8,128)}, f32[2,64,128]{2,1,0:T(8,128)}, f32[128,640]{1,0:T(8,128)}, f32[128,128]{1,0:T(8,128)}) custom-call(f32[2,64,128]{2,1,0:T(8,128)S(1)} %get-tuple-element.8.a, f32[2,64,128]{2,1,0:T(8,128)S(1)} %get-tuple-element.9.b, f32[128,640]{1,0:T(8,128)S(1)} %get-tuple-element.10.c, f32[128,128]{1,0:T(8,128)S(1)} %get-tuple-element.11.d), custom_call_target="tpu_custom_call" | custom-call | tf_op jit(solution)/shard_map/pallas_call | solution.py:517

commit v8 on v7

--- a/solution.py
+++ b/solution.py
@@ -379,13 +379,13 @@
     for h in range(own):
         send5[:, own + h, :] = unstack(dot(d_cols[h], lefts[h], TN))
     exchange(4, send5, recv5)
+    wait_for(recv_sems, 3, recv4.at[pl.ds(0, n // 2 - 1)])
+    early[my_chip, my_core] = jnp.sum(recv4[...], 0) / length
+    spread(8, early)
     gather(3)
     total = grads_of(
         first_ones, block_halves(first_ones), side_by_side(lambda d: factors[d], first_ones)
     )
-    wait_for(recv_sems, 3, recv4.at[pl.ds(0, n // 2 - 1)])
-    early[my_chip, my_core] = jnp.sum(recv4[...], 0) / length
-    spread(8, early)
     for stage in (2, 3):
         for block in came_in(stage):
             ensure(block)

time: 34.5 us -> 34.4 us (level)
  no operation moved by 1% of the time
where the time goes in v8:
time: 34.4 us; the launch traced here: 34.3 us
  Pallas kernels  33.6 us (98%)
  between operations  0.64 us (2%)
    pallas_call x1, Pallas kernels, on_device(): pl.pallas_call(functools.partial(kernel, n_row, n_ch, plan), out_shape=ou...  32.8 us
    pallas_call x1, Pallas kernels, on_device(): pl.pallas_call(write_out, out_shape=out_shape, in_specs=[vmem] * 4, out_s...  0.82 us

profile of v8, /device:TPU:0, one launch (start us, length us, event | category | flops | bytes accessed | tf_op | source)
XLA Modules:
  0.0 34.3 jit_solution(14129803287527278836)
XLA Ops:
  0.6 32.8 %shard_map.138 = (f32[2,64,128]{2,1,0:T(8,128)S(1)}, f32[2,64,128]{2,1,0:T(8,128)S(1)}, f32[128,640]{1,0:T(8,128)S(1)}, f32[128,128]{1,0:T(8,128)S(1)}) custom-call(f32[2,64,128]{2,1,0:T(8,128)} %refs_0_.1, s32[2,64]{1,0:T(2,128)} %refs_1_.1, f32[1,128]{1,0:T(1,128)} %bitcast.7, f32[1,128]{1,0:T(1,128)} %bitcast.8, f32[128,640]{1,0:T(8,128)} %refs_4_.1, ...), custom_call_target="tpu_custom_call" | custom-call | tf_op jit(solution)/shard_map/pallas_call | solution.py:486
  33.5 0.8 %shard_map.139 = (f32[2,64,128]{2,1,0:T(8,128)}, f32[2,64,128]{2,1,0:T(8,128)}, f32[128,640]{1,0:T(8,128)}, f32[128,128]{1,0:T(8,128)}) custom-call(f32[2,64,128]{2,1,0:T(8,128)S(1)} %get-tuple-element.8.a, f32[2,64,128]{2,1,0:T(8,128)S(1)} %get-tuple-element.9.b, f32[128,640]{1,0:T(8,128)S(1)} %get-tuple-element.10.c, f32[128,128]{1,0:T(8,128)S(1)} %get-tuple-element.11.d), custom_call_target="tpu_custom_call" | custom-call | tf_op jit(solution)/shard_map/pallas_call | solution.py:517
